TPU v7x, 32 devices: a whole 2x2x4 slice. The times are simulated.
32 devices in a mesh: grp: 2 (over x), row: 16 (over z, y, core).
Axes of the slice: x: 2, y: 2, z: 4, core: 2. Of those that a mesh axis runs over, the one named last changes fastest.
Arguments:
- tiles: bfloat16 [192, 512, 512], P(('grp', 'row')), may hold values from -0.15625 to 0.15625
- tile_row: int32 [192], P(('grp', 'row')), may hold values from 0 to 63, as said below
- tile_col: int32 [192], P(('grp', 'row')), may hold values from 0 to 63, as said below
- tile_count: int32 [32], P(('grp', 'row')), may hold values from 3 to 6, as said below
- q_block: bfloat16 [32768, 256], P(('grp', 'row')), may hold values from -80 to 80
Outputs:
- q_next: float32 [32768, 256], P(('grp', 'row'))
Inputs may be any that keep to these rules, and one draw needn't show every extreme that they name: `tile_row`: each slot names one of its device's tile rows: d * 2 to d * 2 + 1 for device d. `tile_col`: each slot's tile column is (tile_row + o) mod 64 with o from minus 2 to 2; no two slots of one device name the same pair of tile row and tile column. `tile_count`: some device has all 6 slots live.
All inputs are finite; a program needn't handle non-finite values.
Results may differ from a plain program's by a relative error of at most 0.0029.
Values may be sent and summed in bfloat16 or wider, within the bound.
A program may use at most 64 MiB of HBM per device.

v0:
```python
import jax
import jax.numpy as jnp
from jax import lax
from jax.sharding import PartitionSpec as P

H = 2


def padded_2(block, sides, width):
    for axis, dim in sides:
        count = lax.axis_size(axis)
        forward = [(i, i + 1) for i in range(count - 1)]
        forward.append((count - 1, 0))
        backward = [(target, source) for source, target in forward]
        low = lax.ppermute(
            lax.slice_in_dim(block, block.shape[dim] - width, None, axis=dim), axis, forward
        )
        high = lax.ppermute(lax.slice_in_dim(block, 0, width, axis=dim), axis, backward)
        block = jnp.concatenate([low, block, high], axis=dim)
    return block


def passed_along(block, axis, distance):
    devices = range(lax.axis_size(axis))
    route = [((i - distance) % len(devices), i) for i in devices]
    return lax.ppermute(block, axis, route)


def on_device(tiles, tile_row, tile_col, tile_count, q_block):
    slot_count, tile_size, unused_size = tiles.shape
    basis_width = q_block.shape[1]
    own_tiles = q_block.shape[0] // tile_size
    window = own_tiles + 2 * H
    tile_total = own_tiles * lax.axis_size("grp") * lax.axis_size("row")
    local_row = tile_row % own_tiles
    local_col = (tile_col - tile_row + H) % tile_total + local_row
    padded = padded_2(q_block, ((("grp", "row"), 0),), H * tile_size)
    stack = padded.reshape(window, tile_size, basis_width)
    live_slot = jnp.arange(slot_count, dtype=jnp.int32) < tile_count[0]
    blocks = stack[local_col]
    blocks = jnp.where(live_slot[:, None, None], blocks, jnp.zeros_like(blocks))
    products = jnp.einsum("sab,sbk->sak", tiles, blocks, preferred_element_type=jnp.float32)
    row_ids = jnp.arange(own_tiles, dtype=jnp.int32)
    row_place = ((local_row[None, :] == row_ids[:, None]) & live_slot[None, :]).astype(jnp.float32)
    aq_tiles = jnp.einsum(
        "rs,sak->rak", row_place, products, precision=lax.Precision.HIGHEST
    ).astype(jnp.bfloat16)
    row_part = aq_tiles[local_row]
    images = jnp.einsum("sab,sak->sbk", tiles, row_part, preferred_element_type=jnp.float32)
    column_ids = jnp.arange(window, dtype=jnp.int32)
    col_place = ((local_col[None, :] == column_ids[:, None]) & live_slot[None, :]).astype(
        jnp.float32
    )
    sums = jnp.einsum("cs,sbk->cbk", col_place, images, precision=lax.Precision.HIGHEST)
    own_part = sums[H : H + own_tiles]
    lower = sums[:H].astype(jnp.bfloat16).reshape(H * tile_size, basis_width)
    upper = sums[H + own_tiles :].astype(jnp.bfloat16).reshape(H * tile_size, basis_width)
    from_below = passed_along(upper, ("grp", "row"), 1)
    from_above = passed_along(lower, ("grp", "row"), -1)
    below_tiles = from_below.astype(jnp.float32).reshape(H, tile_size, basis_width)
    above_tiles = from_above.astype(jnp.float32).reshape(H, tile_size, basis_width)
    own_part = own_part + below_tiles
    own_part = own_part + above_tiles
    local_y = own_part.reshape(own_tiles * tile_size, basis_width)
    rows_total = tile_total * tile_size
    local_gram = jnp.dot(
        local_y.T, local_y, precision=lax.Precision.HIGHEST, preferred_element_type=jnp.float32
    )
    gram_matrix = lax.psum(local_gram, ("grp", "row")) / rows_total
    factor_low = jnp.linalg.cholesky(gram_matrix)
    return lax.linalg.triangular_solve(
        factor_low, local_y, left_side=False, lower=True, transpose_a=True
    )


def solution(mesh):
    placed = (
        P(("grp", "row"), None, None),
        P(("grp", "row")),
        P(("grp", "row")),
        P(("grp", "row")),
        P(("grp", "row"), None),
    )
    return jax.shard_map(
        on_device, mesh=mesh, in_specs=placed, out_specs=P(("grp", "row"), None), check_vma=False
    )
```

profile of v0, /device:TPU:0, one launch (start us, length us, event | category | flops | bytes accessed | tf_op | source)
XLA Modules:
  0.0 289.4 jit_solution(1188874127921917125)
XLA Ops:
  6.5 0.5 collective-permute-start
  7.0 5.9 %collective-permute-start.1 = (bf16[1024,256]{1,0:T(8,128)(2,1)}, bf16[1024,256]{1,0:T(8,128)(2,1)S(1)}, u32[]{:S(2)}, u32[]{:S(2)}) collective-permute-start(bf16[1024,256]{1,0:T(8,128)(2,1)} %param.9), channel_id=1, source_target_pairs={{1,0},{2,1},{3,2},{4,3},{5,4},{6,5},{7,6},{8,7},{9,8},{10,9},{11,1... | collective-permute-start | bytes 1572872 | tf_op jit(solution)/shard_map/ppermute | solution.py:18
  12.9 0.7 compare_select_fusion
  14.3 0.7 compare_select_fusion.1
  15.0 5.1 %collective-permute-done = bf16[1024,256]{1,0:T(8,128)(2,1)S(1)} collective-permute-done((bf16[1024,256]{1,0:T(8,128)(2,1)}, bf16[1024,256]{1,0:T(8,128)(2,1)S(1)}, u32[]{:S(2)}, u32[]{:S(2)}) %collective-permute-start) | collective-permute-done | bytes 524320 | tf_op jit(solution)/shard_map/ppermute | solution.py:15
  20.1 2.3 pad_maximum_fusion
  22.4 3.3 %gather_fusion = bf16[6,512,256]{2,1,0:T(8,128)(2,1)} fusion(bf16[6,512,256]{2,1,0:T(8,128)(2,1)} %bitcast.63, s32[1024]{0:T(1024)S(1)} %pad_clamp_fusion.1), kind=kCustom, calls=%fused_computation | custom fusion | bytes 3145752 | tf_op jit(solution)/shard_map/gather | solution.py:40
  25.7 4.3 %convolution_bitcast_fusion.1 = f32[6,512,256]{1,2,0:T(8,128)} fusion(bf16[6,512,512]{2,1,0:T(8,128)(2,1)S(1)} %copy-done, bf16[6,512,256]{2,1,0:T(8,128)(2,1)} %gather_fusion, pred[6]{0:T(512)(128)(4,1)S(1)} %iota_compare_fusion.4), kind=kOutput, calls=%fused_computation.5 | convolution fusion | flops 806092800 | bytes 7864326 | tf_op jit(solution)/shard_map/sab,sbk->sak/dot_general | solution.py:42
  29.9 5.1 %copy.32 = f32[6,512,256]{2,0,1:T(8,128)} copy(f32[6,512,256]{1,2,0:T(8,128)} %convolution_bitcast_fusion.1) | data formatting | bytes 6291456 | tf_op jit(solution)/shard_map/sab,sbk->sak/dot_general | solution.py:42
  35.1 4.3 %convolution_convert_fusion = bf16[2,512,256]{2,0,1:T(2,128)(2,1)S(1)} fusion(f32[6,512,256]{2,0,1:T(8,128)} %copy.32, pred[6]{0:T(512)(128)(4,1)S(1)} %iota_compare_fusion.4, s32[6]{0:T(128)S(1)} %get-tuple-element.22), kind=kOutput, calls=%fused_computation.9 | convolution fusion | flops 19136536 | bytes 3670046 | tf_op jit(solution)/shard_map/rs,sak->rak/dot_general | solution.py:45
  39.4 0.9 copy.33
  40.2 2.9 gather_fusion.1
  43.1 4.1 %convolution_bitcast_fusion = f32[6,512,256]{1,2,0:T(8,128)} fusion(bf16[6,512,256]{2,1,0:T(8,128)(2,1)} %gather_fusion.1, bf16[6,512,512]{2,1,0:T(8,128)(2,1)S(1)} %copy-done), kind=kOutput, calls=%fused_computation.4 | convolution fusion | flops 805306368 | bytes 7864320 | tf_op jit(solution)/shard_map/sab,sak->sbk/dot_general | solution.py:49
  47.2 5.1 %copy.35 = f32[6,512,256]{2,0,1:T(8,128)} copy(f32[6,512,256]{1,2,0:T(8,128)} %convolution_bitcast_fusion) | data formatting | bytes 6291456 | tf_op jit(solution)/shard_map/sab,sak->sbk/dot_general | solution.py:49
  52.3 4.3 %fusion.32 = (bf16[6,512,256]{2,0,1:T(8,128)(2,1)S(1)}, f32[6,512,256]{2,0,1:T(8,128)S(1)}) fusion(f32[6,512,256]{2,0,1:T(8,128)} %copy.35, s32[6]{0:T(128)S(1)} %get-tuple-element.24, pred[6]{0:T(512)(128)(4,1)S(1)} %iota_compare_fusion.4), kind=kOutput, calls=%fused_computation.71 | convolution fusion | flops 57409608 | bytes 7864350 | tf_op jit(solution)/shard_map/cs,sbk->cbk/dot_general | solution.py:54
  56.6 0.7 fusion.31
  57.4 0.1 copy.37
  57.5 4.0 %collective-permute-start.2 = (bf16[1024,256]{1,0:T(8,128)(2,1)S(1)}, bf16[1024,256]{1,0:T(8,128)(2,1)S(1)}, u32[]{:S(2)}, u32[]{:S(2)}) collective-permute-start(bf16[1024,256]{1,0:T(8,128)(2,1)S(1)} %bitcast.64), channel_id=1, source_target_pairs={{31,0},{0,1},{1,2},{2,3},{3,4},{4,5},{5,6},{6,7},{7,8},{8,9},{9,10... | collective-permute-start | bytes 1572872 | tf_op jit(solution)/shard_map/ppermute | solution.py:26
  61.5 0.1 copy.38
  61.6 1.6 collective-permute-start.3
  63.2 0.5 slice.71
  63.7 6.1 %collective-permute-done.2 = bf16[1024,256]{1,0:T(8,128)(2,1)S(1)} collective-permute-done((bf16[1024,256]{1,0:T(8,128)(2,1)S(1)}, bf16[1024,256]{1,0:T(8,128)(2,1)S(1)}, u32[]{:S(2)}, u32[]{:S(2)}) %collective-permute-start.2) | collective-permute-done | bytes 524320 | tf_op jit(solution)/shard_map/ppermute | solution.py:26
  69.9 0.1 fusion.2
  70.0 1.0 copy-done.1
  71.0 2.5 convolution_bitcast_fusion.2
  73.6 132.1 %all-reduce.3.cloned.1.call-done = f32[256,256]{0,1:T(8,128)} async-done(((f32[256,256]{0,1:T(8,128)}), f32[256,256]{0,1:T(8,128)}) %all-reduce.3.cloned.1.call-update) | async-done | bytes 262160 | tf_op jit(solution)/shard_map/psum | solution.py:69
  205.6 1.7 broadcast_multiply_fusion
  207.3 1.1 copy.41
  208.4 1.0 fusion.7
  209.4 0.7 copy-done.3
  210.1 11.7 %cholesky.50 = f32[128,128]{1,0:T(8,128)S(1)} custom-call(f32[128,128]{1,0:T(8,128)S(1)} %cholesky.118), custom_call_target="Cholesky" | custom-call | tf_op jit(solution)/shard_map/jit(cholesky)/cholesky | solution.py:70
  221.9 9.8 %custom-call.14 = f32[1,128,128]{1,2,0:T(8,128)S(1)} custom-call(f32[1,128,128]{2,1,0:T(8,128)S(1)} %get-tuple-element.32), custom_call_target="InvertDiagBlocksLowerTriangular" | custom-call | tf_op jit(solution)/shard_map/jit(cholesky)/cholesky | solution.py:70
  231.7 1.0 constant_dynamic-update-slice_fusion.1
  232.7 1.1 convolution_subtract_fusion
  233.8 11.9 %cholesky.105 = f32[128,128]{1,0:T(8,128)S(1)} custom-call(f32[128,128]{1,0:T(8,128)S(1)} %convolution_subtract_fusion), custom_call_target="Cholesky" | custom-call | tf_op jit(solution)/shard_map/jit(cholesky)/cholesky | solution.py:70
  245.8 0.7 compare_reduce_fusion
  247.8 1.0 select_select_fusion
  248.8 5.3 %while.1 = (s32[]{:T(128)}, f32[256,256]{1,0:T(8,128)S(1)}, s32[2,2]{1,0:T(2,128)S(1)}, f32[2,128,128]{2,1,0:T(8,128)}, s32[]{:T(128)}) while((s32[]{:T(128)}, f32[256,256]{1,0:T(8,128)S(1)}, s32[2,2]{1,0:T(2,128)S(1)}, f32[2,128,128]{2,1,0:T(8,128)}, s32[]{:T(128)}) %tuple.27), condition=%wide.while_cond, body=%wide.while_body.sunk | while | flops 2 | bytes 132705 | solution.py:71
  248.8 0.7 fusion.44
  249.5 2.0 bitcast_dynamic-update-slice_fusion.2
  251.5 0.7 fusion.44
  252.2 2.0 bitcast_dynamic-update-slice_fusion.2
  254.1 20.5 %custom-call.15 = f32[2,128,128]{1,2,0:T(8,128)S(1)} custom-call(f32[2,128,128]{2,1,0:T(8,128)} %get-tuple-element.12), custom_call_target="InvertDiagBlocksLowerTriangular" | custom-call | tf_op jit(solution)/shard_map/triangular_solve | solution.py:71
  274.6 1.7 fusion.5
  276.3 1.0 fusion.8
  277.3 1.7 fusion.4
  279.0 1.0 pad_maximum_fusion.1
  280.0 2.5 copy.42
  (22 shorter events, 0.3 us)
Async XLA Ops:
  6.5 19.2 %copy-start = (bf16[6,512,512]{2,1,0:T(8,128)(2,1)S(1)}, bf16[6,512,512]{2,1,0:T(8,128)(2,1)}, u32[]{:S(2)}) copy-start(bf16[6,512,512]{2,1,0:T(8,128)(2,1)} %param.5) | copy-start | bytes 9437188
  6.5 199.1 %all-reduce.3.cloned.1.call-start = ((), (), s32[]{:S(2)}) async-start(), calls=%async_computation | async-start | bytes 524288 | tf_op jit(solution)/shard_map/psum | solution.py:69
  6.5 13.6 %collective-permute-start = (bf16[1024,256]{1,0:T(8,128)(2,1)}, bf16[1024,256]{1,0:T(8,128)(2,1)S(1)}, u32[]{:S(2)}, u32[]{:S(2)}) collective-permute-start(bf16[1024,256]{1,0:T(8,128)(2,1)} %param.9), channel_id=1, source_target_pairs={{0,1},{1,2},{2,3},{3,4},{4,5},{5,6},{6,7},{7,8},{8,9},{9,10},{10,1... | collective-permute-start | bytes 1572872 | tf_op jit(solution)/shard_map/ppermute | solution.py:15
  7.0 13.1 %collective-permute-start.1 = (bf16[1024,256]{1,0:T(8,128)(2,1)}, bf16[1024,256]{1,0:T(8,128)(2,1)S(1)}, u32[]{:S(2)}, u32[]{:S(2)}) collective-permute-start(bf16[1024,256]{1,0:T(8,128)(2,1)} %param.9), channel_id=1, source_target_pairs={{1,0},{2,1},{3,2},{4,3},{5,4},{6,5},{7,6},{8,7},{9,8},{10,9},{11,1... | collective-permute-start | bytes 1572872 | tf_op jit(solution)/shard_map/ppermute | solution.py:18
  57.5 12.4 %collective-permute-start.2 = (bf16[1024,256]{1,0:T(8,128)(2,1)S(1)}, bf16[1024,256]{1,0:T(8,128)(2,1)S(1)}, u32[]{:S(2)}, u32[]{:S(2)}) collective-permute-start(bf16[1024,256]{1,0:T(8,128)(2,1)S(1)} %bitcast.64), channel_id=1, source_target_pairs={{31,0},{0,1},{1,2},{2,3},{3,4},{4,5},{5,6},{6,7},{7,8},{8,9},{9,10... | collective-permute-start | bytes 1572872 | tf_op jit(solution)/shard_map/ppermute | solution.py:26
  61.6 8.3 %collective-permute-start.3 = (bf16[1024,256]{1,0:T(8,128)(2,1)S(1)}, bf16[1024,256]{1,0:T(8,128)(2,1)S(1)}, u32[]{:S(2)}, u32[]{:S(2)}) collective-permute-start(bf16[1024,256]{1,0:T(8,128)(2,1)S(1)} %bitcast.65), channel_id=1, source_target_pairs={{1,0},{2,1},{3,2},{4,3},{5,4},{6,5},{7,6},{8,7},{9,8},{10,9},{11,1... | collective-permute-start | bytes 1572872 | tf_op jit(solution)/shard_map/ppermute | solution.py:26
  70.0 1.0 copy-start.1
  209.4 0.7 copy-start.3
  245.8 2.0 copy-start.2
Sparse Core Ops, SparseCore 0:
  73.7 131.9 all-reduce.2
where the time goes:
time: 290 us; the launch traced here: 289 us
  waiting for transfers between devices  143 us (49%)
  other arithmetic  63.2 us (22%)
  local copies, waits for them, and re-layouts  29.3 us (10%)
  matrix products  26 us (9%)
  between operations  15.5 us (5%)
  starting transfers between devices  12 us (4%)
    psum x1, waiting for transfers between devices, on_device(): gram_matrix = lax.psum(local_gram, ('grp', 'row')) / rows_total  132 us
    another operation x6, other arithmetic, on_device(): factor_low = jnp.linalg.cholesky(gram_matrix)  34.2 us
    another operation x4, other arithmetic, on_device(): lax.linalg.triangular_solve(factor_low, local_y, left_side=False, lower=T...  22.5 us
    ppermute x2, waiting for transfers between devices, passed_along(): return lax.ppermute(block, axis, route)  6.15 us
    ppermute x1, starting transfers between devices, padded_2(): lax.ppermute(lax.slice_in_dim(block, 0, width, axis=dim), axis, backward)  5.91 us
  transfers between devices with their start and end apart: 5, of which 4 were waited for; matrix products, arithmetic and copies ran while one was open for 1% of the time, Pallas kernels for 0%

commit v1 on v0

--- a/solution.py
+++ b/solution.py
@@ -66,7 +66,7 @@
     local_gram = jnp.dot(
         local_y.T, local_y, precision=lax.Precision.HIGHEST, preferred_element_type=jnp.float32
     )
-    gram_matrix = lax.psum(local_gram, ("grp", "row")) / rows_total
+    gram_matrix = jnp.sum(lax.all_gather(local_gram, ("grp", "row")), axis=0) / rows_total
     factor_low = jnp.linalg.cholesky(gram_matrix)
     return lax.linalg.triangular_solve(
         factor_low, local_y, left_side=False, lower=True, transpose_a=True

time: 290 us -> 243 us (0.84)
  waiting for transfers between devices: 143 us -> 94 us
    psum x1 -> x0, waiting for transfers between devices: 132 us -> none  [on_device(): gram_matrix = lax.psum(local_gram, ('grp', 'row')) / rows_total]
    all_gather x0 -> x1, waiting for transfers between devices: none -> 82.6 us  [on_device(): lax.all_gather(local_gram, ('grp', 'row'))]
    reduce_sum x0 -> x1, other arithmetic: none -> 3.93 us  [on_device(): jnp.sum(lax.all_gather(local_gram, ('grp', 'row')), axis=0) / rows_total]
where the time goes in v1:
time: 243 us; the launch traced here: 242 us
  waiting for transfers between devices  94 us (39%)
  other arithmetic  65.5 us (27%)
  local copies, waits for them, and re-layouts  29.1 us (12%)
  matrix products  26 us (11%)
  between operations  15.5 us (6%)
  starting transfers between devices  12 us (5%)
    all_gather x1, waiting for transfers between devices, on_device(): lax.all_gather(local_gram, ('grp', 'row'))  82.6 us
    another operation x6, other arithmetic, on_device(): factor_low = jnp.linalg.cholesky(gram_matrix)  34.2 us
    another operation x4, other arithmetic, on_device(): lax.linalg.triangular_solve(factor_low, local_y, left_side=False, lower=T...  22.5 us
    ppermute x2, waiting for transfers between devices, passed_along(): return lax.ppermute(block, axis, route)  6.15 us
    ppermute x1, starting transfers between devices, padded_2(): lax.ppermute(lax.slice_in_dim(block, 0, width, axis=dim), axis, backward)  5.91 us
    ppermute x2, starting transfers between devices, passed_along(): return lax.ppermute(block, axis, route)  5.64 us
    another operation x6, local copies, waits for them, and re-layouts  5.28 us
    ppermute x1, waiting for transfers between devices, padded_2(): lax.ppermute(lax.slice_in_dim(block, block.shape[dim] - width, None, axis...  5.14 us
  transfers between devices with their start and end apart: 5, of which 4 were waited for; matrix products, arithmetic and copies ran while one was open for 1% of the time, Pallas kernels for 0%

profile of v1, /device:TPU:0, one launch (start us, length us, event | category | flops | bytes accessed | tf_op | source)
XLA Modules:
  0.0 242.0 jit_solution(8694359249189334284)
XLA Ops:
  6.5 0.5 collective-permute-start
  7.0 5.9 %collective-permute-start.1 = (bf16[1024,256]{1,0:T(8,128)(2,1)}, bf16[1024,256]{1,0:T(8,128)(2,1)S(1)}, u32[]{:S(2)}, u32[]{:S(2)}) collective-permute-start(bf16[1024,256]{1,0:T(8,128)(2,1)} %param.9), channel_id=1, source_target_pairs={{1,0},{2,1},{3,2},{4,3},{5,4},{6,5},{7,6},{8,7},{9,8},{10,9},{11,1... | collective-permute-start | bytes 1572872 | tf_op jit(solution)/shard_map/ppermute | solution.py:18
  12.9 0.7 compare_select_fusion
  14.3 0.7 compare_select_fusion.1
  15.0 5.1 %collective-permute-done = bf16[1024,256]{1,0:T(8,128)(2,1)S(1)} collective-permute-done((bf16[1024,256]{1,0:T(8,128)(2,1)}, bf16[1024,256]{1,0:T(8,128)(2,1)S(1)}, u32[]{:S(2)}, u32[]{:S(2)}) %collective-permute-start) | collective-permute-done | bytes 524320 | tf_op jit(solution)/shard_map/ppermute | solution.py:15
  20.1 2.3 pad_maximum_fusion
  22.4 3.3 %gather_fusion = bf16[6,512,256]{2,1,0:T(8,128)(2,1)} fusion(bf16[6,512,256]{2,1,0:T(8,128)(2,1)} %bitcast.65, s32[1024]{0:T(1024)S(1)} %pad_clamp_fusion.1), kind=kCustom, calls=%fused_computation | custom fusion | bytes 3145752 | tf_op jit(solution)/shard_map/gather | solution.py:40
  25.7 4.3 %convolution_bitcast_fusion.1 = f32[6,512,256]{1,2,0:T(8,128)} fusion(bf16[6,512,512]{2,1,0:T(8,128)(2,1)S(1)} %copy-done, bf16[6,512,256]{2,1,0:T(8,128)(2,1)} %gather_fusion, pred[6]{0:T(512)(128)(4,1)S(1)} %iota_compare_fusion.4), kind=kOutput, calls=%fused_computation.5 | convolution fusion | flops 806092800 | bytes 7864326 | tf_op jit(solution)/shard_map/sab,sbk->sak/dot_general | solution.py:42
  29.9 5.1 %copy.46 = f32[6,512,256]{2,0,1:T(8,128)} copy(f32[6,512,256]{1,2,0:T(8,128)} %convolution_bitcast_fusion.1) | data formatting | bytes 6291456 | tf_op jit(solution)/shard_map/sab,sbk->sak/dot_general | solution.py:42
  35.1 4.3 %convolution_convert_fusion = bf16[2,512,256]{2,0,1:T(2,128)(2,1)S(1)} fusion(f32[6,512,256]{2,0,1:T(8,128)} %copy.46, pred[6]{0:T(512)(128)(4,1)S(1)} %iota_compare_fusion.4, s32[6]{0:T(128)S(1)} %get-tuple-element.22), kind=kOutput, calls=%fused_computation.9 | convolution fusion | flops 19136536 | bytes 3670046 | tf_op jit(solution)/shard_map/rs,sak->rak/dot_general | solution.py:45
  39.4 0.9 copy.47
  40.2 2.9 %gather_fusion.1 = bf16[6,512,256]{2,1,0:T(8,128)(2,1)} fusion(bf16[2,512,256]{2,1,0:T(8,128)(2,1)} %copy.47, s32[1024]{0:T(1024)S(1)} %pad_clamp_fusion), kind=kCustom, calls=%fused_computation.1 | custom fusion | bytes 3145752 | tf_op jit(solution)/shard_map/gather | solution.py:48
  43.1 4.1 %convolution_bitcast_fusion = f32[6,512,256]{1,2,0:T(8,128)} fusion(bf16[6,512,256]{2,1,0:T(8,128)(2,1)} %gather_fusion.1, bf16[6,512,512]{2,1,0:T(8,128)(2,1)S(1)} %copy-done), kind=kOutput, calls=%fused_computation.4 | convolution fusion | flops 805306368 | bytes 7864320 | tf_op jit(solution)/shard_map/sab,sak->sbk/dot_general | solution.py:49
  47.2 5.1 %copy.49 = f32[6,512,256]{2,0,1:T(8,128)} copy(f32[6,512,256]{1,2,0:T(8,128)} %convolution_bitcast_fusion) | data formatting | bytes 6291456 | tf_op jit(solution)/shard_map/sab,sak->sbk/dot_general | solution.py:49
  52.3 4.3 %fusion.32 = (bf16[6,512,256]{2,0,1:T(8,128)(2,1)S(1)}, f32[6,512,256]{2,0,1:T(8,128)S(1)}) fusion(f32[6,512,256]{2,0,1:T(8,128)} %copy.49, s32[6]{0:T(128)S(1)} %get-tuple-element.24, pred[6]{0:T(512)(128)(4,1)S(1)} %iota_compare_fusion.4), kind=kOutput, calls=%fused_computation.70 | convolution fusion | flops 57409608 | bytes 7864350 | tf_op jit(solution)/shard_map/cs,sbk->cbk/dot_general | solution.py:54
  56.6 0.7 fusion.31
  57.4 0.1 copy.51
  57.5 4.0 %collective-permute-start.2 = (bf16[1024,256]{1,0:T(8,128)(2,1)S(1)}, bf16[1024,256]{1,0:T(8,128)(2,1)S(1)}, u32[]{:S(2)}, u32[]{:S(2)}) collective-permute-start(bf16[1024,256]{1,0:T(8,128)(2,1)S(1)} %bitcast.66), channel_id=1, source_target_pairs={{31,0},{0,1},{1,2},{2,3},{3,4},{4,5},{5,6},{6,7},{7,8},{8,9},{9,10... | collective-permute-start | bytes 1572872 | tf_op jit(solution)/shard_map/ppermute | solution.py:26
  61.5 0.1 copy.52
  61.6 1.6 collective-permute-start.3
  63.2 0.5 slice.71
  63.7 6.1 %collective-permute-done.2 = bf16[1024,256]{1,0:T(8,128)(2,1)S(1)} collective-permute-done((bf16[1024,256]{1,0:T(8,128)(2,1)S(1)}, bf16[1024,256]{1,0:T(8,128)(2,1)S(1)}, u32[]{:S(2)}, u32[]{:S(2)}) %collective-permute-start.2) | collective-permute-done | bytes 524320 | tf_op jit(solution)/shard_map/ppermute | solution.py:26
  69.9 0.1 fusion.2
  70.0 1.0 copy-done.1
  71.0 2.6 %convolution_bitcast_fusion.2 = f32[256,256]{1,0:T(8,128)} fusion(f32[2,512,256]{2,1,0:T(8,128)S(1)} %fusion.2), kind=kOutput, calls=%fused_computation.10 | convolution fusion | flops 805306368 | bytes 1310720 | tf_op jit(solution)/shard_map/dot_general | solution.py:66
  73.6 82.6 %all-gather.3.cloned.1.call-done = f32[8192,256]{1,0:T(8,128)} async-done(((f32[256,256]{1,0:T(8,128)}), f32[8192,256]{1,0:T(8,128)}) %all-gather.3.cloned.1.call-update) | async-done | bytes 8388624 | tf_op jit(solution)/shard_map/all_gather | solution.py:69
  156.3 3.9 %reduce_sum.11 = f32[256,256]{1,0:T(8,128)S(1)} reduce(f32[32,256,256]{2,1,0:T(8,128)} %bitcast.64, f32[]{:T(128)} %constant.107.clone.1), dimensions={0}, to_apply=%region_0.1 | reduce | flops 2031616 | bytes 8650756 | tf_op jit(solution)/shard_map/reduce_sum | solution.py:69
  160.2 0.8 copy.54
  161.0 1.0 fusion.7
  162.0 0.7 copy-done.3
  162.7 11.7 %cholesky.50 = f32[128,128]{1,0:T(8,128)S(1)} custom-call(f32[128,128]{1,0:T(8,128)S(1)} %cholesky.118), custom_call_target="Cholesky" | custom-call | tf_op jit(solution)/shard_map/jit(cholesky)/cholesky | solution.py:70
  174.5 9.8 %custom-call.14 = f32[1,128,128]{1,2,0:T(8,128)S(1)} custom-call(f32[1,128,128]{2,1,0:T(8,128)S(1)} %get-tuple-element.32), custom_call_target="InvertDiagBlocksLowerTriangular" | custom-call | tf_op jit(solution)/shard_map/jit(cholesky)/cholesky | solution.py:70
  184.3 1.0 constant_dynamic-update-slice_fusion.1
  185.4 1.1 convolution_subtract_fusion
  186.5 11.9 %cholesky.105 = f32[128,128]{1,0:T(8,128)S(1)} custom-call(f32[128,128]{1,0:T(8,128)S(1)} %convolution_subtract_fusion), custom_call_target="Cholesky" | custom-call | tf_op jit(solution)/shard_map/jit(cholesky)/cholesky | solution.py:70
  198.4 0.7 compare_reduce_fusion
  200.4 1.0 select_select_fusion
  201.5 5.3 %while.1 = (s32[]{:T(128)}, f32[256,256]{1,0:T(8,128)S(1)}, s32[2,2]{1,0:T(2,128)S(1)}, f32[2,128,128]{2,1,0:T(8,128)}, s32[]{:T(128)}) while((s32[]{:T(128)}, f32[256,256]{1,0:T(8,128)S(1)}, s32[2,2]{1,0:T(2,128)S(1)}, f32[2,128,128]{2,1,0:T(8,128)}, s32[]{:T(128)}) %tuple.27), condition=%wide.while_cond, body=%wide.while_body.sunk | while | flops 2 | bytes 132705 | solution.py:71
  201.5 0.7 fusion.44
  202.1 2.0 bitcast_dynamic-update-slice_fusion.2
  204.1 0.7 fusion.44
  204.8 2.0 bitcast_dynamic-update-slice_fusion.2
  206.7 20.5 %custom-call.15 = f32[2,128,128]{1,2,0:T(8,128)S(1)} custom-call(f32[2,128,128]{2,1,0:T(8,128)} %get-tuple-element.12), custom_call_target="InvertDiagBlocksLowerTriangular" | custom-call | tf_op jit(solution)/shard_map/triangular_solve | solution.py:71
  227.2 1.7 fusion.5
  228.9 1.0 fusion.8
  229.9 1.7 fusion.4
  231.6 1.0 pad_maximum_fusion.1
  232.6 2.5 %copy.55 = f32[1024,256]{1,0:T(8,128)} copy(f32[1024,256]{0,1:T(8,128)} %pad_maximum_fusion.1) | data formatting | bytes 2097152 | tf_op jit(solution)/shard_map/triangular_solve | solution.py:71
  (22 shorter events, 0.3 us)
Async XLA Ops:
  6.5 19.2 %copy-start = (bf16[6,512,512]{2,1,0:T(8,128)(2,1)S(1)}, bf16[6,512,512]{2,1,0:T(8,128)(2,1)}, u32[]{:S(2)}) copy-start(bf16[6,512,512]{2,1,0:T(8,128)(2,1)} %param.5) | copy-start | bytes 9437188
  6.5 149.7 %all-gather.3.cloned.1.call-start = ((), (), s32[]{:S(2)}) async-start(), calls=%async_computation | async-start | bytes 8650752 | tf_op jit(solution)/shard_map/all_gather | solution.py:69
  6.5 13.6 %collective-permute-start = (bf16[1024,256]{1,0:T(8,128)(2,1)}, bf16[1024,256]{1,0:T(8,128)(2,1)S(1)}, u32[]{:S(2)}, u32[]{:S(2)}) collective-permute-start(bf16[1024,256]{1,0:T(8,128)(2,1)} %param.9), channel_id=1, source_target_pairs={{0,1},{1,2},{2,3},{3,4},{4,5},{5,6},{6,7},{7,8},{8,9},{9,10},{10,1... | collective-permute-start | bytes 1572872 | tf_op jit(solution)/shard_map/ppermute | solution.py:15
  7.0 13.1 %collective-permute-start.1 = (bf16[1024,256]{1,0:T(8,128)(2,1)}, bf16[1024,256]{1,0:T(8,128)(2,1)S(1)}, u32[]{:S(2)}, u32[]{:S(2)}) collective-permute-start(bf16[1024,256]{1,0:T(8,128)(2,1)} %param.9), channel_id=1, source_target_pairs={{1,0},{2,1},{3,2},{4,3},{5,4},{6,5},{7,6},{8,7},{9,8},{10,9},{11,1... | collective-permute-start | bytes 1572872 | tf_op jit(solution)/shard_map/ppermute | solution.py:18
  57.5 12.4 %collective-permute-start.2 = (bf16[1024,256]{1,0:T(8,128)(2,1)S(1)}, bf16[1024,256]{1,0:T(8,128)(2,1)S(1)}, u32[]{:S(2)}, u32[]{:S(2)}) collective-permute-start(bf16[1024,256]{1,0:T(8,128)(2,1)S(1)} %bitcast.66), channel_id=1, source_target_pairs={{31,0},{0,1},{1,2},{2,3},{3,4},{4,5},{5,6},{6,7},{7,8},{8,9},{9,10... | collective-permute-start | bytes 1572872 | tf_op jit(solution)/shard_map/ppermute | solution.py:26
  61.6 8.3 %collective-permute-start.3 = (bf16[1024,256]{1,0:T(8,128)(2,1)S(1)}, bf16[1024,256]{1,0:T(8,128)(2,1)S(1)}, u32[]{:S(2)}, u32[]{:S(2)}) collective-permute-start(bf16[1024,256]{1,0:T(8,128)(2,1)S(1)} %bitcast.67), channel_id=1, source_target_pairs={{1,0},{2,1},{3,2},{4,3},{5,4},{6,5},{7,6},{8,7},{9,8},{10,9},{11,1... | collective-permute-start | bytes 1572872 | tf_op jit(solution)/shard_map/ppermute | solution.py:26
  70.0 1.0 copy-start.1
  162.0 0.7 copy-start.3
  198.4 2.0 copy-start.2
Sparse Core Ops, SparseCore 0:
  73.7 82.5 all-gather.2
